TPU v7x, 32 devices: a whole 2x2x4 slice. The times are simulated.
32 devices in a mesh: dp: 2 (over x), tp: 4 (over z), ep: 4 (over y, core).
Axes of the slice: x: 2, y: 2, z: 4, core: 2. Of those that a mesh axis runs over, the one named last changes fastest.
Arguments:
- tokens: bfloat16 [8, 32, 2048], P(('dp', 'ep')), parts along dimension 0
- topk_idx: int32 [8, 32, 8], P(('dp', 'ep')), parts along dimension 0
- ln1_gain: bfloat16 [2048], replicated
- w_qkv: bfloat16 [2048, 16, 3, 128], P(None, 'tp')
- w_out: bfloat16 [2048, 2048], P('tp')
- ln2_gain: bfloat16 [2048], replicated
- w_router: bfloat16 [2048, 64], replicated
- w_gate: bfloat16 [64, 2048, 1024], P('ep', None, 'tp')
- w_up: bfloat16 [64, 2048, 1024], P('ep', None, 'tp')
- w_down: bfloat16 [64, 1024, 2048], P('ep', 'tp')
Outputs:
- output: bfloat16 [8, 32, 2048], P(('dp', 'ep')), parts along dimension 0
There are 2 independent parts. A program takes and returns all parts, laid end to end along the dimension named above; an argument that names none is the same for every part.
All inputs are finite; a program needn't handle non-finite values.
Results may differ from a plain program's by a relative error of at most 0.00897813.
Values are sent between devices in bfloat16 or wider.
A program may use at most 1 GiB of HBM per device.

v0:
```python
import jax
import jax.numpy as jnp
from jax import lax
from jax.sharding import PartitionSpec as P

ROPE_BASE = 500000.0
CLIP_QKV = 8.0
NORM_EPS = 1e-5


def layer_norm(values_in, gain_vec):
    mean_val = jnp.mean(values_in, axis=-1, keepdims=True)
    centered = values_in - mean_val
    var_val = jnp.mean(centered * centered, axis=-1, keepdims=True)
    return (centered * lax.rsqrt(var_val + NORM_EPS) * gain_vec.astype(jnp.float32)).astype(jnp.bfloat16)


def apply_rope(values_in, cos_tab, sin_tab):
    half_dim = values_in.shape[-1] // 2
    first_half = values_in[..., :half_dim]
    second_half = values_in[..., half_dim:]
    return jnp.concatenate([first_half * cos_tab - second_half * sin_tab, second_half * cos_tab + first_half * sin_tab], axis=-1)


def attention_block(tokens, ln1_gain, w_qkv, w_out):
    n_prompt, length, hidden = tokens.shape
    n_kv = w_qkv.shape[1]
    group_cols = w_qkv.shape[2]
    head_dim = w_qkv.shape[3]
    group = group_cols - 2
    normed = layer_norm(tokens.reshape(n_prompt * length, hidden).astype(jnp.float32), ln1_gain)
    qkv_all = jnp.dot(normed, w_qkv.reshape(hidden, n_kv * group_cols * head_dim), preferred_element_type=jnp.float32).astype(jnp.bfloat16)
    qkv_all = jnp.clip(qkv_all, -CLIP_QKV, CLIP_QKV).reshape(n_prompt, length, n_kv, group_cols, head_dim)
    inv_freq = ROPE_BASE ** (-jnp.arange(head_dim // 2, dtype=jnp.float32) * (2.0 / head_dim))
    angles = jnp.arange(length, dtype=jnp.float32)[:, None] * inv_freq[None, :]
    cos_tab = jnp.cos(angles)
    sin_tab = jnp.sin(angles)
    query_rot = apply_rope(qkv_all[:, :, :, :group].astype(jnp.float32), cos_tab[:, None, None, :], sin_tab[:, None, None, :]).astype(jnp.bfloat16)
    key_rot = apply_rope(qkv_all[:, :, :, group].astype(jnp.float32), cos_tab[:, None, :], sin_tab[:, None, :]).astype(jnp.bfloat16)
    value_rows = qkv_all[:, :, :, group + 1]
    scores = jnp.einsum("bqgrd,bkgd->bgrqk", query_rot, key_rot, preferred_element_type=jnp.float32) * head_dim ** -0.5
    causal = jnp.arange(length)[:, None] >= jnp.arange(length)[None, :]
    probs = jax.nn.softmax(jnp.where(causal, scores, -1e30), axis=-1).astype(jnp.bfloat16)
    mixed = jnp.einsum("bgrqk,bkgd->bqgrd", probs, value_rows, preferred_element_type=jnp.float32).astype(jnp.bfloat16)
    return jnp.dot(mixed.reshape(n_prompt * length, n_kv * group * head_dim), w_out, preferred_element_type=jnp.float32)


def route_weights(normed, w_router, choice):
    probs_all = jax.nn.softmax(jnp.dot(normed, w_router, preferred_element_type=jnp.float32), axis=-1)
    picked = jnp.take_along_axis(probs_all, choice, axis=-1)
    return picked / jnp.sum(picked, axis=-1, keepdims=True)


def slot_table(choice, n_exp, capacity):
    tok_count, top_k = choice.shape
    flat_choice = choice.reshape(-1)
    hit_mask = (flat_choice[:, None] == jnp.arange(n_exp, dtype=jnp.int32)[None, :]).astype(jnp.int32)
    slot_rank = jnp.sum((jnp.cumsum(hit_mask, axis=0) - 1) * hit_mask, axis=1)
    slot_ids = flat_choice * capacity + slot_rank
    owners = jnp.full((n_exp * capacity,), tok_count, jnp.int32).at[slot_ids].set(jnp.arange(tok_count * top_k, dtype=jnp.int32) // top_k)
    return slot_ids.reshape(tok_count, top_k), owners


def expert_mlp(rows_in, w_gate, w_up, w_down):
    gate_act = jnp.einsum("secd,edf->secf", rows_in, w_gate, preferred_element_type=jnp.float32)
    up_act = jnp.einsum("secd,edf->secf", rows_in, w_up, preferred_element_type=jnp.float32)
    hidden_act = (jax.nn.silu(gate_act) * up_act).astype(jnp.bfloat16)
    return jnp.einsum("secf,efd->secd", hidden_act, w_down, preferred_element_type=jnp.float32)


def tp_reduce_scatter(part_sum, axis_pos):
    got_rows = lax.all_to_all(part_sum.astype(jnp.bfloat16), "tp", axis_pos, axis_pos)
    return jnp.sum(got_rows.astype(jnp.float32), axis=axis_pos)


def solution(mesh):
    tp_size = mesh.shape["tp"]
    ep_size = mesh.shape["ep"]

    def device_step(tokens, topk_idx, ln1_gain, w_qkv, w_out, ln2_gain, w_router, w_gate, w_up, w_down):
        n_prompt, length, hidden = tokens.shape
        top_k = topk_idx.shape[-1]
        n_exp = w_router.shape[1]
        tok_dev = n_prompt * length
        own_rows = tok_dev // tp_size
        capacity = 3 * tok_dev * top_k // (2 * n_exp)
        row_start = lax.axis_index("tp") * own_rows
        attn_part = attention_block(tokens, ln1_gain, w_qkv, w_out)
        attn_own = tp_reduce_scatter(attn_part.reshape(tp_size, own_rows, hidden), 0)
        tok_own = lax.dynamic_slice_in_dim(tokens.reshape(tok_dev, hidden), row_start, own_rows, 0)
        resid_own = tok_own.astype(jnp.float32) + attn_own
        normed_own = layer_norm(resid_own, ln2_gain)
        normed = lax.all_gather(normed_own, "tp", axis=0, tiled=True)
        choice = topk_idx.reshape(tok_dev, top_k)
        slot_ids, owners = slot_table(choice, n_exp, capacity)
        send_rows = jnp.take(normed, owners, axis=0, mode="fill", fill_value=0).reshape(ep_size, n_exp // ep_size * capacity, hidden)
        recv_rows = lax.all_to_all(send_rows, "ep", 0, 0).reshape(ep_size, n_exp // ep_size, capacity, hidden)
        expert_part = expert_mlp(recv_rows, w_gate, w_up, w_down)
        expert_own = tp_reduce_scatter(expert_part.reshape(tp_size, -1, hidden), 0)
        expert_rows = lax.all_gather(expert_own.astype(jnp.bfloat16), "tp", axis=0, tiled=True)
        back_rows = lax.all_to_all(expert_rows.reshape(ep_size, -1, hidden), "ep", 0, 0).reshape(n_exp * capacity, hidden)
        choice_own = lax.dynamic_slice_in_dim(choice, row_start, own_rows, 0)
        slot_own = lax.dynamic_slice_in_dim(slot_ids, row_start, own_rows, 0)
        weights = route_weights(normed_own, w_router, choice_own)
        picked = jnp.take(back_rows, slot_own.reshape(-1), axis=0).reshape(own_rows, top_k, hidden)
        out_own = (resid_own + jnp.sum(picked.astype(jnp.float32) * weights[:, :, None], axis=1)).astype(jnp.bfloat16)
        layer_out = lax.all_gather(out_own, "tp", axis=0, tiled=True)
        return layer_out.reshape(n_prompt, length, hidden)

    tok_spec = P(("dp", "ep"), None, None)
    in_specs = (tok_spec, tok_spec, P(None), P(None, "tp", None, None), P("tp", None), P(None), P(None, None), P("ep", None, "tp"), P("ep", None, "tp"), P("ep", "tp", None))
    return jax.shard_map(device_step, mesh=mesh, in_specs=in_specs, out_specs=tok_spec, check_vma=False)
```

profile of v0, /device:TPU:0, one launch (start us, length us, event | category | flops | bytes accessed | tf_op | source)
XLA Modules:
  0.0 226.5 jit_solution(10370891714534851629)
XLA Ops:
  6.6 1.2 convert_reduce_fusion
  7.7 1.1 fusion.26
  8.9 10.7 %copy.61 = bf16[2048,4,3,128]{0,3,2,1:T(8,128)(2,1)} copy(bf16[2048,4,3,128]{3,1,2,0:T(4,128)(2,1)} %param.13) | data formatting | bytes 12582912 | tf_op args[3]
  19.6 4.8 %fusion.12 = bf16[32,1536]{1,0:T(8,128)(2,1)S(1)} fusion(bf16[2048,1536]{0,1:T(8,128)(2,1)} %bitcast.146, bf16[1,32,2048]{2,1,0:T(8,128)(2,1)S(1)} %copy-done.2, f32[2048]{0:T(1024)S(1)} %convert_element_type.107, f32[32]{0:T(128)S(1)} %add_rsqrt_fusion.1, f32[32]{0:T(128)S(1)} %broadcast_multiply_fusion.2), kind=kOutput, calls=%fused_computation.14 | convolution fusion | flops 201752576 | bytes 6529280 | tf_op jit(solution)/shard_map/dot_general | solution.py:32
  24.5 0.1 fusion.64
  24.7 0.1 fusion.51
  24.8 0.1 fusion.37
  24.9 0.1 fusion.39
  25.0 0.2 fusion.65
  25.2 0.2 fusion.16
  25.5 1.1 convolution_convert_fusion.1
  26.6 6.4 %all-to-all-start = ((bf16[4,8,2048]{2,1,0:T(8,128)(2,1)}), bf16[4,8,2048]{2,1,0:T(8,128)(2,1)S(1)}, u32[]{:S(2)}, u32[]{:S(2)}) async-start(bf16[4,8,2048]{2,1,0:T(8,128)(2,1)} %convolution_convert_fusion.1), calls=%async_computation | async-start | bytes 262144 | tf_op jit(solution)/shard_map/all_to_all | solution.py:72
  33.1 0.1 eq.29
  33.2 0.1 eq.25
  33.3 0.6 reduce-window.6
  33.9 0.2 slice_reduce_fusion
  34.1 0.1 mul.281
  34.2 0.1 fusion.34
  34.4 1.4 scatter_custom_fusion
  35.8 0.1 broadcast_in_dim.61
  35.9 3.6 %all-to-all-done = bf16[4,8,2048]{2,1,0:T(8,128)(2,1)S(1)} async-done(((bf16[4,8,2048]{2,1,0:T(8,128)(2,1)}), bf16[4,8,2048]{2,1,0:T(8,128)(2,1)S(1)}, u32[]{:S(2)}, u32[]{:S(2)}) %all-to-all-start) | async-done | bytes 131104 | tf_op jit(solution)/shard_map/all_to_all | solution.py:72
  39.5 0.1 fusion.63
  39.6 0.2 multiply_reduce_fusion.1
  39.9 0.1 multiply_convert_fusion
  39.9 13.6 %all_gather.9 = bf16[32,2048]{1,0:T(8,128)(2,1)S(1)} all-gather(bf16[8,2048]{1,0:T(8,128)(2,1)S(1)} %multiply_convert_fusion), channel_id=1, replica_groups=mesh['dp'=2,'tp'=4,'ep'=4] {'tp'}, dimensions={0}, use_global_device_ids=true | all-gather | bytes 163840 | tf_op jit(solution)/shard_map/all_gather | solution.py:93
  53.6 2.4 %gather_fusion = bf16[384,2048]{1,0:T(8,128)(2,1)S(1)} fusion(bf16[32,2048]{1,0:T(8,128)(2,1)S(1)} %all_gather.9, s32[1024]{0:T(1024)S(1)} %pad_clamp_fusion.1), kind=kCustom, calls=%fused_computation | custom fusion | bytes 3147264 | tf_op jit(solution)/shard_map/jit(_take)/gather | solution.py:96
  56.0 0.2 broadcast_select_fusion
  56.2 22.6 %all_to_all.20 = bf16[4,96,2048]{2,1,0:T(8,128)(2,1)S(1)} all-to-all(bf16[4,96,2048]{2,1,0:T(8,128)(2,1)S(1)} %broadcast_select_fusion), channel_id=1, replica_groups=mesh['dp'=2,'tp'=4,'ep'=4] {'ep'}, dimensions={0} | all-to-all | bytes 3145728 | tf_op jit(solution)/shard_map/all_to_all | solution.py:97
  78.8 1.2 copy.71
  80.1 8.6 %fusion.2 = f32[16,4,6,256]{3,1,2,0:T(4,128)S(1)} fusion(bf16[4,16,6,2048]{3,0,2,1:T(4,128)(2,1)S(1)} %bitcast.150, bf16[16,2048,256]{2,1,0:T(8,128)(2,1)} %param.18), kind=kOutput, calls=%fused_computation.6 | convolution fusion | flops 402653184 | bytes 18743296 | tf_op jit(solution)/shard_map/secd,edf->secf/dot_general | solution.py:66
  88.7 8.6 %fusion.4 = f32[16,4,6,256]{3,1,2,0:T(4,128)S(1)} fusion(bf16[4,16,6,2048]{3,0,2,1:T(4,128)(2,1)S(1)} %bitcast.151, bf16[16,2048,256]{2,1,0:T(8,128)(2,1)} %param.17), kind=kOutput, calls=%fused_computation.8 | convolution fusion | flops 402653184 | bytes 18743296 | tf_op jit(solution)/shard_map/secd,edf->secf/dot_general | solution.py:65
  97.3 0.3 fusion.17
  97.6 2.3 %fusion.9 = bf16[4,16,6,2048]{3,2,0,1:T(8,128)(2,1)S(1)} fusion(bf16[16,256,2048]{2,1,0:T(8,128)(2,1)S(1)} %bitcast.145, bf16[4,16,6,256]{3,1,2,0:T(8,128)(2,1)S(1)} %fusion.17), kind=kOutput, calls=%fused_computation.11 | convolution fusion | flops 403439616 | bytes 18546688 | tf_op jit(solution)/shard_map/secf,efd->secd/dot_general | solution.py:68
  99.9 1.3 copy.75
  101.3 0.9 copy.76
  102.2 39.3 %all_to_all.21 = bf16[4,96,2048]{2,1,0:T(8,128)(2,1)S(1)} all-to-all(bf16[4,96,2048]{2,1,0:T(8,128)(2,1)S(1)} %copy.76), channel_id=1, replica_groups=mesh['dp'=2,'tp'=4,'ep'=4] {'tp'}, dimensions={0} | all-to-all | bytes 3145728 | tf_op jit(solution)/shard_map/all_to_all | solution.py:72
  141.5 1.1 reduce_sum.115
  142.9 35.3 %all-gather.2.cloned.1.call-done = bf16[384,2048]{1,0:T(8,128)(2,1)} async-done(((bf16[96,2048]{1,0:T(8,128)(2,1)}), bf16[384,2048]{1,0:T(8,128)(2,1)}) %all-gather.2.cloned.1.call-update) | async-done | bytes 1572880 | tf_op jit(solution)/shard_map/all_gather | solution.py:100
  178.2 4.3 %all-to-all-start.3 = ((bf16[4,96,2048]{2,1,0:T(8,128)(2,1)}), bf16[4,96,2048]{2,1,0:T(8,128)(2,1)}, u32[]{:S(2)}, u32[]{:S(2)}) async-start(bf16[4,96,2048]{2,1,0:T(8,128)(2,1)} %bitcast.149), calls=%async_computation.3 | async-start | bytes 3145728 | tf_op jit(solution)/shard_map/all_to_all | solution.py:101
  182.6 0.3 fusion.66
  182.9 0.2 fusion.56
  183.2 0.7 gather_fusion.2
  184.0 0.1 fusion.61
  184.2 18.2 %all-to-all-done.3 = bf16[4,96,2048]{2,1,0:T(8,128)(2,1)} async-done(((bf16[4,96,2048]{2,1,0:T(8,128)(2,1)}), bf16[4,96,2048]{2,1,0:T(8,128)(2,1)}, u32[]{:S(2)}, u32[]{:S(2)}) %all-to-all-start.3) | async-done | bytes 1572896 | tf_op jit(solution)/shard_map/all_to_all | solution.py:101
  202.4 2.6 %gather_fusion.1 = bf16[64,2048]{1,0:T(8,128)(2,1)S(1)} fusion(bf16[384,2048]{1,0:T(8,128)(2,1)} %bitcast.34, s32[1024]{0:T(1024)S(1)} %pad_clamp_fusion), kind=kCustom, calls=%fused_computation.1 | custom fusion | bytes 524544 | tf_op jit(solution)/shard_map/jit(_take)/gather | solution.py:105
  205.0 0.4 multiply_reduce_fusion
  205.4 13.6 %all_gather.11 = bf16[32,2048]{1,0:T(8,128)(2,1)S(1)} all-gather(bf16[8,2048]{1,0:T(8,128)(2,1)S(1)} %add_convert_fusion), channel_id=1, replica_groups=mesh['dp'=2,'tp'=4,'ep'=4] {'tp'}, dimensions={0}, use_global_device_ids=true | all-gather | bytes 163840 | tf_op jit(solution)/shard_map/all_gather | solution.py:107
  219.0 0.7 copy.98
  (61 shorter events, 1.0 us)
Async XLA Ops:
  6.5 19.0 %copy-start = (bf16[512,2048]{1,0:T(8,128)(2,1)S(1)}, bf16[512,2048]{1,0:T(8,128)(2,1)}, u32[]{:S(2)}) copy-start(bf16[512,2048]{1,0:T(8,128)(2,1)} %param.14) | copy-start | bytes 6291460
  8.9 10.7 %copy-start.4 = (bf16[2048]{0:T(1024)(128)(2,1)S(1)}, bf16[2048]{0:T(1024)(128)(2,1)}, u32[]{:S(2)}) copy-start(bf16[2048]{0:T(1024)(128)(2,1)} %param.12) | copy-start | bytes 12292
  8.9 10.7 %copy-start.2 = (bf16[1,32,2048]{2,1,0:T(8,128)(2,1)S(1)}, bf16[1,32,2048]{2,1,0:T(8,128)(2,1)}, u32[]{:S(2)}) copy-start(bf16[1,32,2048]{2,1,0:T(8,128)(2,1)} %param.10) | copy-start | bytes 393220
  24.5 8.5 %copy-start.5 = (s32[1,32,8]{1,2,0:T(8,128)S(1)}, s32[1,32,8]{1,2,0:T(8,128)}, u32[]{:S(2)}) copy-start(s32[1,32,8]{1,2,0:T(8,128)} %param.11) | copy-start | bytes 3076
  24.8 11.0 %copy-start.6 = (bf16[2048]{0:T(1024)(128)(2,1)S(1)}, bf16[2048]{0:T(1024)(128)(2,1)}, u32[]{:S(2)}) copy-start(bf16[2048]{0:T(1024)(128)(2,1)} %param.15) | copy-start | bytes 12292
  26.6 12.8 %all-to-all-start = ((bf16[4,8,2048]{2,1,0:T(8,128)(2,1)}), bf16[4,8,2048]{2,1,0:T(8,128)(2,1)S(1)}, u32[]{:S(2)}, u32[]{:S(2)}) async-start(bf16[4,8,2048]{2,1,0:T(8,128)(2,1)} %convolution_convert_fusion.1), calls=%async_computation | async-start | bytes 262144 | tf_op jit(solution)/shard_map/all_to_all | solution.py:72
  33.0 145.2 %all-gather.2.cloned.1.call-start = ((), (), s32[]{:S(2)}) async-start(), calls=%async_computation.4 | async-start | bytes 1966080 | tf_op jit(solution)/shard_map/all_gather | solution.py:100
  80.1 17.5 %slice-start = ((s8[16777216]{0:T(1024)(128)(4,1)}), s8[4194304]{0:T(1024)(128)(4,1)S(1)}, s32[]{:S(2)}) async-start(s8[16777216]{0:T(1024)(128)(4,1)} %bitcast.144), calls=%async_computation.5 | async-start | bytes 8388608
  80.1 17.5 %slice-start.1 = ((s8[16777216]{0:T(1024)(128)(4,1)}), s8[4194304]{0:T(1024)(128)(4,1)S(1)}, s32[]{:S(2)}) async-start(s8[16777216]{0:T(1024)(128)(4,1)} %bitcast.144), calls=%async_computation.6 | async-start | bytes 8388608
  88.7 8.9 %slice-start.2 = ((s8[16777216]{0:T(1024)(128)(4,1)}), s8[4194304]{0:T(1024)(128)(4,1)S(1)}, s32[]{:S(2)}) async-start(s8[16777216]{0:T(1024)(128)(4,1)} %bitcast.144), calls=%async_computation.7 | async-start | bytes 8388608
  88.7 8.9 %slice-start.3 = ((s8[16777216]{0:T(1024)(128)(4,1)}), s8[4194304]{0:T(1024)(128)(4,1)S(1)}, s32[]{:S(2)}) async-start(s8[16777216]{0:T(1024)(128)(4,1)} %bitcast.144), calls=%async_computation.8 | async-start | bytes 8388608
  142.6 40.0 %copy-start.3 = (bf16[2048,64]{0,1:T(8,128)(2,1)S(1)}, bf16[2048,64]{0,1:T(8,128)(2,1)}, u32[]{:S(2)}) copy-start(bf16[2048,64]{0,1:T(8,128)(2,1)} %param.16) | copy-start | bytes 786436
  178.2 24.1 %all-to-all-start.3 = ((bf16[4,96,2048]{2,1,0:T(8,128)(2,1)}), bf16[4,96,2048]{2,1,0:T(8,128)(2,1)}, u32[]{:S(2)}, u32[]{:S(2)}) async-start(bf16[4,96,2048]{2,1,0:T(8,128)(2,1)} %bitcast.149), calls=%async_computation.3 | async-start | bytes 3145728 | tf_op jit(solution)/shard_map/all_to_all | solution.py:101
  183.2 36.5 %copy-start.1 = (bf16[512,2048]{1,0:T(8,128)(2,1)S(1)}, bf16[512,2048]{1,0:T(8,128)(2,1)}, u32[]{:S(2)}) copy-start(bf16[512,2048]{1,0:T(8,128)(2,1)} %param.14) | copy-start | bytes 6291460
Sparse Core Ops, SparseCore 0:
  142.7 35.4 all-gather.1
where the time goes:
time: 227 us
  blocking collectives  89.2 us (39%)
  waiting for transfers between devices  57.1 us (25%)
  matrix products  26.1 us (11%)
  local copies, waits for them, and re-layouts  23.2 us (10%)
  between operations  13.8 us (6%)
  starting transfers between devices  10.7 us (5%)
  other arithmetic  6.39 us (3%)
    all_to_all x1, blocking collectives, tp_reduce_scatter(): lax.all_to_all(part_sum.astype(jnp.bfloat16), 'tp', axis_pos, axis_pos)  39.3 us
    all_gather x1, waiting for transfers between devices, device_step(): lax.all_gather(expert_own.astype(jnp.bfloat16), 'tp', axis=0, tiled=True)  35.3 us
    all_to_all x1, blocking collectives, device_step(): lax.all_to_all(send_rows, 'ep', 0, 0)  22.6 us
    all_to_all x1, waiting for transfers between devices, device_step(): lax.all_to_all(expert_rows.reshape(ep_size, -1, hidden), 'ep', 0, 0)  18.2 us
    all_gather x1, blocking collectives, device_step(): layer_out = lax.all_gather(out_own, 'tp', axis=0, tiled=True)  13.6 us
    all_gather x1, blocking collectives, device_step(): normed = lax.all_gather(normed_own, 'tp', axis=0, tiled=True)  13.6 us
    unnamed x25, local copies, waits for them, and re-layouts  11.5 us
    dot_general x1, matrix products, expert_mlp(): jnp.einsum('secd,edf->secf', rows_in, w_gate, preferred_element_type=jnp....  8.58 us
  transfers between devices with their start and end apart: 3, of which 3 were waited for; matrix products, arithmetic and copies ran while one was open for 2% of the time, Pallas kernels for 0%

commit v1 on v0

v1 whole, which is shorter than its diff:
```python
import functools

import jax
import jax.numpy as jnp
import numpy as np
from jax import lax
from jax.experimental import pallas as pl
from jax.experimental.pallas import tpu as pltpu
from jax.sharding import PartitionSpec as P

ROPE_BASE = 500000.0
CLIP_QKV = 8.0
NORM_EPS = 1e-5
F32 = jnp.float32
BF16 = jnp.bfloat16
MESH = pl.DeviceIdType.MESH

LANES = 128
KTILE = 256
QKV_CHUNKS = 4
OUT_BLOCKS = 4


def normalize(rows, gain_ref):
    mean_val = jnp.mean(rows, axis=-1, keepdims=True)
    centered = rows - mean_val
    var_val = jnp.mean(centered * centered, axis=-1, keepdims=True)
    inv_std = lax.rsqrt(var_val + NORM_EPS)
    for blk in range(rows.shape[-1] // LANES):
        cols = slice(blk * LANES, (blk + 1) * LANES)
        gain_row = gain_ref[blk : blk + 1, :].astype(F32)
        yield blk, (centered[:, cols] * inv_std * gain_row).astype(BF16)


def layer_kernel(
    x_ref, x3_ref, topk_ref, gain1_ref, gain2_ref, cos_ref, sin_ref,
    wqkv_hbm, wout_hbm, wr_hbm, wg_hbm, wu_hbm, wd_hbm,
    out_ref,
    wqkv, wout, wr, wg, wu, wd, lhs, part_f32, part_send, part_recv, g_all, x1_own, topk_all,
    coef, acc, c1_send, c1_recv, c2_send, c2_recv, c3_send, c3_recv, y_all,
    wq_sem, wm_sem, wg_sem, wu_sem, wd_sem,
    rs_ss, rs_rs, g_ss, g_rs, tk_ss, tk_rs, c1_ss, c1_rs, c2_ss, c2_rs, c3_ss, c3_rs, y_ss, y_rs,
):
    z = lax.axis_index("tp")
    ep = lax.axis_index("ep")
    core = lax.rem(ep, 2)
    ypos = ep // 2
    partner = ep + 1 - 2 * core
    across = lax.rem(ep + 2, 4)
    diagonal = lax.rem(partner + 2, 4)
    z_order = [lax.rem(z + d, 4) for d in (2, 1, 3)]
    n_loc = wg.shape[0]
    hidden = x_ref.shape[1]
    rows_dev = x_ref.shape[0]
    heads = wqkv.shape[2]

    barrier = pltpu.get_barrier_semaphore()
    for zp in z_order:
        pl.semaphore_signal(barrier, inc=1, device_id={"tp": zp}, device_id_type=MESH)
    for other in (partner, across, diagonal):
        pl.semaphore_signal(barrier, inc=1, device_id={"ep": other}, device_id_type=MESH)

    chunk_rows = hidden // QKV_CHUNKS
    loads_qkv = []
    for ch in range(QKV_CHUNKS):
        for kind in range(3):
            rows = pl.ds(ch * chunk_rows, chunk_rows)
            loads_qkv.append(pltpu.make_async_copy(wqkv_hbm.at[rows, kind], wqkv.at[kind, rows], wq_sem.at[ch * 3 + kind]))
    for copy in loads_qkv:
        copy.start()
    load_wout = pltpu.make_async_copy(wout_hbm, wout, wm_sem.at[0])
    load_wout.start()
    load_wr = pltpu.make_async_copy(wr_hbm, wr, wm_sem.at[1])
    load_wr.start()

    def load_gate(e):
        return pltpu.make_async_copy(wg_hbm.at[e], wg.at[e], wg_sem.at[e])

    def load_up(e):
        return pltpu.make_async_copy(wu_hbm.at[e], wu.at[e], wu_sem.at[e])

    def load_down(e):
        return pltpu.make_async_copy(wd_hbm.at[e], wd.at[e], wd_sem.at[e])

    for e in range(n_loc):
        load_gate(e).start()
        load_up(e).start()
    for e in range(n_loc):
        load_down(e).start()

    tokens_f32 = x_ref[...].astype(F32)
    spread_row = lax.broadcasted_iota(jnp.int32, (LANES, heads * LANES), 0)
    spread_col = lax.broadcasted_iota(jnp.int32, (LANES, heads * LANES), 1)
    spread = (lax.shift_right_logical(spread_col, 2) == spread_row).astype(BF16)
    lane_head = lax.rem(lax.broadcasted_iota(jnp.int32, (rows_dev, heads * LANES), 1), heads)
    for blk, normed in normalize(tokens_f32, gain1_ref):
        wide = jnp.dot(normed, spread, preferred_element_type=F32)
        for h in range(heads):
            picked = jnp.where(lane_head == h, wide, 0.0).astype(BF16)
            for part in range(2):
                lhs[2 * blk + part, h * rows_dev : (h + 1) * rows_dev, :] = picked[:, part * KTILE : (part + 1) * KTILE]

    wqkv_rows = wqkv.reshape(3, hidden * heads, LANES)
    tiles = hidden * heads // KTILE // QKV_CHUNKS
    qkv = [None, None, None]
    for ch in range(QKV_CHUNKS):
        for kind in range(3):
            loads_qkv[ch * 3 + kind].wait()
        for kt in range(ch * tiles, (ch + 1) * tiles):
            left = lhs[kt]
            for kind in range(3):
                term = jnp.dot(left, wqkv_rows[kind, kt * KTILE : (kt + 1) * KTILE, :], preferred_element_type=F32)
                qkv[kind] = term if qkv[kind] is None else qkv[kind] + term
    qkv = [jnp.clip(v.astype(BF16), -CLIP_QKV, CLIP_QKV) for v in qkv]

    cos_tab = jnp.concatenate([cos_ref[...]] * heads, axis=0)
    sin_tab = jnp.concatenate([sin_ref[...]] * heads, axis=0)

    def rope(v):
        wide = v.astype(F32)
        return (wide * cos_tab + pltpu.roll(wide, LANES // 2, 1) * sin_tab).astype(BF16)

    scores = lax.dot_general(rope(qkv[0]), rope(qkv[1]), (((1,), (1,)), ((), ())), preferred_element_type=F32)
    scores = scores * LANES ** -0.5
    q_pos = lax.broadcasted_iota(jnp.int32, scores.shape, 0)
    k_pos = lax.broadcasted_iota(jnp.int32, scores.shape, 1)
    same_head = lax.shift_right_logical(q_pos, 5) == lax.shift_right_logical(k_pos, 5)
    scores = jnp.where(same_head & (q_pos >= k_pos), scores, -1e30)
    scores = jnp.exp(scores - jnp.max(scores, axis=-1, keepdims=True))
    probs = (scores / jnp.sum(scores, axis=-1, keepdims=True)).astype(BF16)
    mixed = jnp.dot(probs, qkv[2], preferred_element_type=F32).astype(BF16)
    mixed = jnp.concatenate([mixed[h * rows_dev : (h + 1) * rows_dev] for h in range(heads)], axis=1)
    load_wout.wait()
    attn = jnp.dot(mixed, wout[...], preferred_element_type=F32)
    for zp in range(4):
        piece = attn[zp * 8 : (zp + 1) * 8]
        part_f32[zp] = piece
        part_send[zp] = piece.astype(BF16)

    pl.semaphore_wait(barrier, 6)

    def rs_copy(d, zp):
        return pltpu.make_async_remote_copy(part_send.at[zp], part_recv.at[z], rs_ss.at[d], rs_rs.at[z], device_id={"tp": zp}, device_id_type=MESH)

    rs_sends = [rs_copy(d, zp) for d, zp in enumerate(z_order)]
    for copy in rs_sends:
        copy.start()
    tk_sends = []
    for d, other in enumerate((partner, across, diagonal)):
        copy = pltpu.make_async_remote_copy(topk_ref, topk_all.at[ep], tk_ss.at[d], tk_rs.at[ep], device_id={"ep": other}, device_id_type=MESH)
        copy.start()
        tk_sends.append(copy)
    topk_all[ep] = topk_ref[...]

    x1 = x3_ref[z].astype(F32)
    total = part_f32[z]
    for zp in (z_order[1], z_order[2], z_order[0]):
        pltpu.make_async_remote_copy(part_send.at[zp], part_recv.at[zp], rs_ss.at[0], rs_rs.at[zp], device_id={"tp": zp}, device_id_type=MESH).wait_recv()
        total = total + part_recv[zp].astype(F32)
    x1 = x1 + total
    x1_own[...] = x1
    for blk, normed in normalize(x1, gain2_ref):
        g_all[ep * 4 + z, :, blk * LANES : (blk + 1) * LANES] = normed

    g_sends = []

    def send_piece(e, zp, **device):
        piece = e * 4 + zp
        copy = pltpu.make_async_remote_copy(g_all.at[piece], g_all.at[piece], g_ss.at[len(g_sends)], g_rs.at[piece], device_id=device, device_id_type=MESH)
        copy.start()
        g_sends.append(copy)

    def wait_piece(e, zp):
        piece = e * 4 + zp
        pltpu.make_async_remote_copy(g_all.at[piece], g_all.at[piece], g_ss.at[0], g_rs.at[piece], device_id={"tp": z_order[0]}, device_id_type=MESH).wait_recv()

    for zp in z_order:
        send_piece(ep, z, tp=zp)
    send_piece(ep, z, ep=across)
    send_piece(ep, z, ep=partner)
    near = [z, z_order[1], z_order[2], z_order[0]]
    for i, zp in enumerate(near):
        if i > 0:
            wait_piece(ep, zp)
            send_piece(ep, zp, ep=across)
            send_piece(ep, zp, ep=partner)
    for zp in near:
        wait_piece(across, zp)
        send_piece(across, zp, ep=partner)
    for e in (partner, diagonal):
        for zp in near:
            wait_piece(e, zp)
    k_tiles = hidden // KTILE
    for kt in range(k_tiles):
        lhs[n_loc + kt] = jnp.concatenate([g_all[p, :, kt * KTILE : (kt + 1) * KTILE] for p in range(16)], axis=0)

    def over_g(dot_tile):
        total = dot_tile(lhs[n_loc], slice(0, KTILE))
        for kt in range(1, k_tiles):
            total = total + dot_tile(lhs[n_loc + kt], slice(kt * KTILE, (kt + 1) * KTILE))
        return total


    for other in (partner, across, diagonal):
        pltpu.make_async_remote_copy(topk_ref, topk_all.at[other], tk_ss.at[0], tk_rs.at[other], device_id={"ep": other}, device_id_type=MESH).wait_recv()
    load_wr.wait()
    logits = over_g(lambda g, ks: lax.dot_general(wr[:, ks], g, (((1,), (1,)), ((), ())), preferred_element_type=F32))
    logits = jnp.exp(logits - jnp.max(logits, axis=0, keepdims=True))
    route = logits / jnp.sum(logits, axis=0, keepdims=True)
    choice = jnp.concatenate([topk_all[e] for e in range(4)], axis=1)
    expert_id = lax.broadcasted_iota(jnp.int32, route.shape, 0)
    chosen = expert_id == choice[0:1, :]
    for k in range(1, choice.shape[0]):
        chosen = chosen | (expert_id == choice[k : k + 1, :])
    route = jnp.where(chosen, route, 0.0)
    route = route / jnp.sum(route, axis=0, keepdims=True)
    coef[0 : route.shape[0], :] = route
    local = coef[pl.ds(pl.multiple_of(ep * n_loc, 8), n_loc), :]
    local = jnp.concatenate([local, jnp.zeros((LANES - n_loc, LANES), F32)], axis=0)
    coef[...] = local.T

    def up_step(e, carry):
        load_gate(e).wait()
        load_up(e).wait()
        gate_act = over_g(lambda g, ks: jnp.dot(g, wg[e, ks, :], preferred_element_type=F32))
        up_act = over_g(lambda g, ks: jnp.dot(g, wu[e, ks, :], preferred_element_type=F32))
        lhs[e] = (gate_act * jax.nn.sigmoid(gate_act) * up_act).astype(BF16)
        return carry

    lax.fori_loop(0, n_loc, up_step, 0, unroll=2)
    for e in range(n_loc):
        load_down(e).wait()

    width = hidden // OUT_BLOCKS

    def down_block(nb):
        for half in range(width // KTILE):
            cols = slice(nb * width + half * KTILE, nb * width + (half + 1) * KTILE)
            total = None
            for e in range(n_loc):
                term = jnp.dot(lhs[e], wd[e, :, cols], preferred_element_type=F32) * coef[:, e : e + 1]
                total = term if total is None else total + term
            for e in range(4):
                acc[nb, e, :, half * KTILE : (half + 1) * KTILE] = total[e * rows_dev : (e + 1) * rows_dev]

    def c1_copy(nb):
        return pltpu.make_async_remote_copy(c1_send.at[nb], c1_recv.at[nb], c1_ss.at[nb], c1_rs.at[nb], device_id={"ep": partner}, device_id_type=MESH)

    def c2_copy(nb):
        return pltpu.make_async_remote_copy(c2_send.at[nb], c2_recv.at[nb], c2_ss.at[nb], c2_rs.at[nb], device_id={"ep": across}, device_id_type=MESH)

    def c3_copy(nb, d, zp):
        return pltpu.make_async_remote_copy(c3_send.at[nb, zp], c3_recv.at[nb, z], c3_ss.at[nb * 3 + d], c3_rs.at[nb * 4 + z], device_id={"tp": zp}, device_id_type=MESH)

    def y_copy(nb, d, zp):
        return pltpu.make_async_remote_copy(y_all.at[nb, z], y_all.at[nb, z], y_ss.at[nb * 3 + d], y_rs.at[nb * 4 + z], device_id={"tp": zp}, device_id_type=MESH)

    def stage1(nb):
        for yp in range(2):
            c1_send[nb, yp] = acc[nb, 2 * yp + 1 - core].astype(BF16)
        c1_copy(nb).start()

    def stage2(nb):
        c1_copy(nb).wait_recv()
        c2_send[nb] = (acc[nb, 2 * (1 - ypos) + core] + c1_recv[nb, 1 - ypos].astype(F32)).astype(BF16)
        c2_copy(nb).start()

    def stage3(nb):
        c2_copy(nb).wait_recv()
        total = acc[nb, ep] + c1_recv[nb, ypos].astype(F32) + c2_recv[nb].astype(F32)
        for zp in range(4):
            part_f32[zp, :, nb * width : (nb + 1) * width] = total[zp * 8 : (zp + 1) * 8]
            c3_send[nb, zp] = total[zp * 8 : (zp + 1) * 8].astype(BF16)
        for d, zp in enumerate(z_order):
            c3_copy(nb, d, zp).start()

    def stage4(nb):
        cols = slice(nb * width, (nb + 1) * width)
        total = part_f32[z, :, cols]
        for zp in (z_order[1], z_order[2], z_order[0]):
            pltpu.make_async_remote_copy(c3_send.at[nb, zp], c3_recv.at[nb, zp], c3_ss.at[nb * 3], c3_rs.at[nb * 4 + zp], device_id={"tp": zp}, device_id_type=MESH).wait_recv()
            total = total + c3_recv[nb, zp].astype(F32)
        y_all[nb, z] = (x1_own[:, cols] + total).astype(BF16)
        for d, zp in enumerate(z_order):
            y_copy(nb, d, zp).start()

    def stage5(nb):
        for zp in (z_order[1], z_order[2], z_order[0]):
            pltpu.make_async_remote_copy(y_all.at[nb, zp], y_all.at[nb, zp], y_ss.at[nb * 3], y_rs.at[nb * 4 + zp], device_id={"tp": zp}, device_id_type=MESH).wait_recv()
        for zp in range(4):
            out_ref[zp, :, nb * width : (nb + 1) * width] = y_all[nb, zp]

    stages = [stage2, stage3, stage4, stage5]
    for step in range(OUT_BLOCKS + len(stages)):
        if step < OUT_BLOCKS:
            down_block(step)
            stage1(step)
        for lag, stage in enumerate(stages):
            nb = step - 1 - lag
            if 0 <= nb < OUT_BLOCKS:
                stage(nb)

    for copy in rs_sends + tk_sends + g_sends:
        copy.wait_send()
    for nb in range(OUT_BLOCKS):
        c1_copy(nb).wait_send()
        c2_copy(nb).wait_send()
        for d, zp in enumerate(z_order):
            c3_copy(nb, d, zp).wait_send()
            y_copy(nb, d, zp).wait_send()


def solution(mesh):
    def device_step(tokens, topk_idx, ln1_gain, w_qkv, w_out, ln2_gain, w_router, w_gate, w_up, w_down):
        rows_dev = tokens.shape[0] * tokens.shape[1]
        length, hidden = tokens.shape[1:]
        n_exp = w_router.shape[1]
        n_loc, _, ffn = w_gate.shape
        top_k = topk_idx.shape[-1]
        heads, head_dim = w_qkv.shape[1], w_qkv.shape[3]
        width = hidden // OUT_BLOCKS
        inv_freq = ROPE_BASE ** (-np.arange(head_dim // 2, dtype=np.float32) * np.float32(2.0 / head_dim))
        angles = np.arange(length, dtype=np.float32)[:, None] * inv_freq[None, :].astype(np.float32)
        cos_tab = np.concatenate([np.cos(angles)] * 2, axis=1).astype(np.float32)
        sin_tab = np.concatenate([-np.sin(angles), np.sin(angles)], axis=1).astype(np.float32)
        vmem = pl.BlockSpec(memory_space=pltpu.VMEM)
        hbm = pl.BlockSpec(memory_space=pl.ANY)
        dma = pltpu.SemaphoreType.DMA
        nb = OUT_BLOCKS
        y = pl.pallas_call(
            layer_kernel,
            name="moe_layer",
            out_shape=jax.ShapeDtypeStruct((4, 8, hidden), BF16),
            in_specs=[vmem] * 7 + [hbm] * 6,
            out_specs=vmem,
            scratch_shapes=[
                pltpu.VMEM((3, hidden, heads, head_dim), BF16),
                pltpu.VMEM((heads * head_dim, hidden), BF16),
                pltpu.VMEM((n_exp, hidden), BF16),
                pltpu.VMEM((n_loc, hidden, ffn), BF16),
                pltpu.VMEM((n_loc, hidden, ffn), BF16),
                pltpu.VMEM((n_loc, ffn, hidden), BF16),
                pltpu.VMEM((hidden * heads // KTILE, heads * rows_dev, KTILE), BF16),
                pltpu.VMEM((4, 8, hidden), F32),
                pltpu.VMEM((4, 8, hidden), BF16),
                pltpu.VMEM((4, 8, hidden), BF16),
                pltpu.VMEM((16, 8, hidden), BF16),
                pltpu.VMEM((8, hidden), F32),
                pltpu.VMEM((4, top_k, rows_dev), jnp.int32),
                pltpu.VMEM((LANES, LANES), F32),
                pltpu.VMEM((nb, 4, rows_dev, width), F32),
                pltpu.VMEM((nb, 2, rows_dev, width), BF16),
                pltpu.VMEM((nb, 2, rows_dev, width), BF16),
                pltpu.VMEM((nb, rows_dev, width), BF16),
                pltpu.VMEM((nb, rows_dev, width), BF16),
                pltpu.VMEM((nb, 4, 8, width), BF16),
                pltpu.VMEM((nb, 4, 8, width), BF16),
                pltpu.VMEM((nb, 4, 8, width), BF16),
                dma((QKV_CHUNKS * 3,)), dma((2,)), dma((n_loc,)), dma((n_loc,)), dma((n_loc,)),
                dma((3,)), dma((4,)), dma((15,)), dma((16,)), dma((3,)), dma((4,)),
                dma((nb,)), dma((nb,)), dma((nb,)), dma((nb,)),
                dma((3 * nb,)), dma((4 * nb,)), dma((3 * nb,)), dma((4 * nb,)),
            ],
            compiler_params=pltpu.CompilerParams(collective_id=0, has_side_effects=True, vmem_limit_bytes=67043328),
        )(
            tokens.reshape(rows_dev, hidden),
            tokens.reshape(4, 8, hidden),
            topk_idx.reshape(rows_dev, top_k).T,
            ln1_gain.reshape(hidden // LANES, LANES),
            ln2_gain.reshape(hidden // LANES, LANES),
            jnp.asarray(cos_tab),
            jnp.asarray(sin_tab),
            jnp.transpose(w_qkv, (0, 2, 1, 3)),
            w_out,
            w_router.T,
            w_gate,
            w_up,
            w_down,
        )
        return y.reshape(tokens.shape)

    tok_spec = P(("dp", "ep"), None, None)
    in_specs = (tok_spec, tok_spec, P(None), P(None, "tp", None, None), P("tp", None), P(None), P(None, None), P("ep", None, "tp"), P("ep", None, "tp"), P("ep", "tp", None))
    return jax.shard_map(device_step, mesh=mesh, in_specs=in_specs, out_specs=tok_spec, check_vma=False)
```

time: 227 us -> 68.2 us (0.30)
  blocking collectives: 89.2 us -> 0 us
  Pallas kernels: 0 us -> 66.5 us
  waiting for transfers between devices: 57.1 us -> 0 us
  matrix products: 26.1 us -> 0 us
  local copies, waits for them, and re-layouts: 23.2 us -> 1.57 us
  between operations: 13.8 us -> 0.01 us
  starting transfers between devices: 10.7 us -> 0 us
  other arithmetic: 6.39 us -> 0 us
    pallas_call x0 -> x1, Pallas kernels: none -> 66.5 us  [device_step(): pl.pallas_call(layer_kernel, name='moe_layer', out_shape=jax.ShapeDtypeSt...]
    all_to_all x2 -> x0, blocking collectives: 62 us -> none  [the longest x1 39.3 us: tp_reduce_scatter(): lax.all_to_all(part_sum.astype(jnp.bfloat16), 'tp', axis_pos, axis_pos)]
    all_gather x1 -> x0, waiting for transfers between devices: 35.3 us -> none  [device_step(): lax.all_gather(expert_own.astype(jnp.bfloat16), 'tp', axis=0, tiled=True)]
    all_gather x2 -> x0, blocking collectives: 27.2 us -> none  [the longest x1 13.6 us: device_step(): layer_out = lax.all_gather(out_own, 'tp', axis=0, tiled=True)]
    dot_general x8 -> x0, matrix products: 26.1 us -> none  [the longest x1 8.58 us: expert_mlp(): jnp.einsum('secd,edf->secf', rows_in, w_gate, preferred_element_type=jnp....]
    all_to_all x2 -> x0, waiting for transfers between devices: 21.7 us -> none  [the longest x1 18.2 us: device_step(): lax.all_to_all(expert_rows.reshape(ep_size, -1, hidden), 'ep', 0, 0)]
    all_to_all x2 -> x0, starting transfers between devices: 10.7 us -> none  [the longest x1 6.38 us: tp_reduce_scatter(): lax.all_to_all(part_sum.astype(jnp.bfloat16), 'tp', axis_pos, axis_pos)]
    unnamed x25 -> x1, local copies, waits for them, and re-layouts: 11.5 us -> 1.57 us
  transfers between devices with their start and end apart: 3 -> 0, of which waited for: 3 -> 0; matrix products, arithmetic and copies ran while one was open for 2% -> 0% of each run, Pallas kernels for 0% -> 0%
where the time goes in v1:
time: 68.2 us; the launch traced here: 68 us
  Pallas kernels  66.5 us (98%)
  local copies, waits for them, and re-layouts  1.57 us (2%)
    pallas_call x1, Pallas kernels, device_step(): pl.pallas_call(layer_kernel, name='moe_layer', out_shape=jax.ShapeDtypeSt...  66.5 us
    unnamed x1, local copies, waits for them, and re-layouts  1.57 us

profile of v1, /device:TPU:0, one launch (start us, length us, event | category | flops | bytes accessed | tf_op | source)
XLA Modules:
  0.0 68.0 jit_solution(12298546520725644253)
XLA Ops:
  0.0 66.5 %moe_layer.1 = bf16[4,8,2048]{2,1,0:T(8,128)(2,1)} custom-call(bf16[32,2048]{1,0:T(8,128)(2,1)} %bitcast.11, bf16[4,8,2048]{2,1,0:T(8,128)(2,1)} %bitcast.12, s32[8,32]{1,0:T(8,128)} %bitcast.15, bf16[16,128]{1,0:T(8,128)(2,1)} %bitcast.16, bf16[16,128]{1,0:T(8,128)(2,1)} %bitcast.17, f32[32,128]{1,0:T(8,128)} %constant.4.clone.cos_ref, ...), custom_call_target="tpu_custom_call" | custom-call | tf_op jit(solution)/shard_map/moe_layer/pallas_call | solution.py:330
  66.5 1.6 %copy.14 = bf16[1,32,2048]{2,1,0:T(8,128)(2,1)} copy(bf16[1,32,2048]{2,1,0:T(8,128)(2,1)} %bitcast.13) | data formatting | bytes 262144
